TPU v7x, 32 devices: a whole 2x2x4 slice. The times are simulated.
32 devices in a mesh: grp: 4 (over x, core), dev: 8 (over z, y).
Axes of the slice: x: 2, y: 2, z: 4, core: 2. Of those that a mesh axis runs over, the one named last changes fastest.
Arguments:
- points: bfloat16 [65536, 1024], P(('grp', 'dev')), may hold values from -6 to 6
- blocks: int32 [65536, 1], P(('grp', 'dev')), may hold values from 0 to 63; in each aligned block of 2048 rows (0 to 2047, 2048 to 4095, ...) at most 64 rows name the same one
- finals: int32 [65536], P(('grp', 'dev')), may hold values from 0 to 255
- centroids: bfloat16 [16384, 1024], P('dev'), may hold values from -6 to 6
Outputs:
- distances: bfloat16 [65536, 256], P(('grp', 'dev'))
- refreshed_centroids: float32 [16384, 1024], P('dev', 'grp')
Inputs may be any that keep to these rules, and one draw needn't show every extreme that they name: `blocks`: among the 2048 rows of one device no block is named by more than 64 rows, and some block by exactly 64. Block b is held by index b // 8 of dev. The point's centroid is row 256 * blocks + finals of centroids.
All inputs are finite; a program needn't handle non-finite values.
Results may differ from a plain program's by a relative error of at most 0.008.
Values may be sent and summed in bfloat16 or wider, within the bound.
A program may use at most 128 MiB of HBM per device.

v0:
```python
import jax
import jax.numpy as jnp
from jax import lax
from jax.sharding import PartitionSpec as P

BS = 256


def block_work(received_points, wanted, centroid_table, width, block_size):
    cent_norm = jnp.sum(jnp.square(centroid_table.astype(jnp.float32)), axis=-1)
    row_norm = jnp.sum(jnp.square(received_points.astype(jnp.float32)), axis=-1)
    cross_products = jnp.einsum(
        "nzy,nvy->nzv", received_points, centroid_table, preferred_element_type=jnp.float32
    )
    dists = ((row_norm[:, :, None] - 2.0 * cross_products + cent_norm[:, None, :]) / width).astype(
        jnp.bfloat16
    )
    onehot_assign = wanted[:, :, None] == jnp.arange(block_size, dtype=jnp.int32)[None, None, :]
    sums = jnp.einsum(
        "xnt,xni->xti",
        onehot_assign.astype(jnp.bfloat16),
        received_points,
        preferred_element_type=jnp.float32,
    )
    counts = jnp.sum(onehot_assign.astype(jnp.float32), axis=1)
    return (dists, sums, counts)


def shards(points, blocks, finals, centroids):
    shard_counts = lax.axis_size("dev")
    count_grp = lax.axis_size("grp")
    npoints, width = points.shape
    block_size = BS
    owned = centroids.shape[0] // block_size
    nblocks = owned * shard_counts
    depth = 2 * npoints // nblocks
    block_ids = blocks[:, 0]
    labels = jnp.arange(nblocks, dtype=jnp.int32)
    member = block_ids[:, None] == labels[None, :]
    lower = (jnp.arange(npoints)[:, None] > jnp.arange(npoints)[None, :]).astype(jnp.bfloat16)
    before = jnp.dot(lower, member.astype(jnp.bfloat16), preferred_element_type=jnp.float32)
    ranks = jnp.sum(jnp.where(member, before, 0.0), axis=1).astype(jnp.int32)
    share = width // count_grp
    slots = block_ids * depth + ranks
    outgoing = jnp.zeros((nblocks * depth, width), jnp.bfloat16).at[slots].set(points)
    targets = jnp.full((nblocks * depth,), -1, jnp.int32).at[slots].set(finals)
    outgoing = outgoing.reshape(nblocks, depth, width)
    targets = targets.reshape(nblocks, depth)
    received_points, wanted = (
        lax.all_to_all(outgoing, "dev", split_axis=0, concat_axis=1, tiled=True),
        lax.all_to_all(targets, "dev", split_axis=0, concat_axis=1, tiled=True),
    )
    centroid_table = centroids.reshape(owned, block_size, width)
    dists, sums, counts = block_work(received_points, wanted, centroid_table, width, block_size)
    sums = sums.reshape(owned * block_size, width)
    counts = counts.reshape(owned * block_size)
    returned = lax.all_to_all(dists, "dev", split_axis=1, concat_axis=0, tiled=True)
    distances = returned.reshape(nblocks * depth, block_size)[slots]
    col_sums = lax.psum_scatter(
        sums.astype(jnp.bfloat16), "grp", scatter_dimension=1, tiled=True
    ).astype(jnp.float32)
    all_counts = lax.psum(counts, "grp")
    own_cols = lax.dynamic_slice_in_dim(centroids, lax.axis_index("grp") * share, share, 1).astype(
        jnp.float32
    )
    refreshed_centroids = (col_sums + own_cols) / (all_counts + 1.0)[:, None]
    return (distances, refreshed_centroids)


def solution(mesh):
    placed = (P(("grp", "dev"), None), P(("grp", "dev"), None), P(("grp", "dev")), P("dev", None))
    return jax.shard_map(
        shards,
        mesh=mesh,
        in_specs=placed,
        out_specs=(P(("grp", "dev"), None), P("dev", "grp")),
        check_vma=False,
    )
```

profile of v0, /device:TPU:0, one launch (start us, length us, event | category | flops | bytes accessed | tf_op | source)
XLA Modules:
  0.0 339.8 jit_solution(2973195217341700019)
XLA Ops:
  7.2 0.0 copy-start.1
  7.2 2.5 fusion.7
  9.6 0.0 copy-done.1
  9.7 8.2 %scatter_custom_fusion.1 = s32[4096]{0:T(1024)S(1)} fusion(s32[2048]{0:T(1024)S(1)} %bitcast.28, s32[2048]{0:T(1024)} %param.6, s32[]{:T(128)} %constant.8.clone.1), kind=kCustom, calls=%fused_computation.21 | custom fusion | bytes 16896 | tf_op jit(solution)/shard_map/scatter | solution.py:46
  17.9 0.1 all_to_all.43
  18.0 0.7 reshape.73
  18.7 7.3 %all-to-all-start.2 = ((s32[8,1,512]{2,1,0:T(1,128)}), s32[8,1,512]{2,1,0:T(1,128)S(1)}, u32[]{:S(2)}, u32[]{:S(2)}) async-start(s32[8,1,512]{2,1,0:T(1,128)} %reshape.73), calls=%async_computation.2 | async-start | bytes 32768 | tf_op jit(solution)/shard_map/all_to_all | solution.py:51
  26.0 15.2 %scatter_custom_fusion = bf16[4096,1024]{1,0:T(8,128)(2,1)} fusion(s32[2048]{0:T(1024)S(1)} %bitcast.29, bf16[2048,1024]{1,0:T(8,128)(2,1)} %param.4, bf16[]{:T(256)} %constant.12.clone.1), kind=kCustom, calls=%fused_computation.11 | custom fusion | bytes 8389120 | tf_op jit(solution)/shard_map/scatter | solution.py:45
  41.2 0.0 all-to-all-done.2
  41.2 6.0 %all-to-all-start = ((bf16[64,64,1024]{2,1,0:T(8,128)(2,1)}), bf16[64,64,1024]{2,1,0:T(8,128)(2,1)}, u32[]{:S(2)}, u32[]{:S(2)}) async-start(bf16[64,64,1024]{2,1,0:T(8,128)(2,1)} %bitcast.21), calls=%async_computation | async-start | bytes 16777216 | tf_op jit(solution)/shard_map/all_to_all | solution.py:50
  47.2 0.2 reduce-scatter.2.cloned.1.call-start
  47.5 0.5 broadcast.19
  48.0 0.7 reduce.2
  48.7 0.1 reshape.74
  48.8 0.1 eq.34
  48.8 181.0 %all-to-all-done = bf16[64,64,1024]{2,1,0:T(8,128)(2,1)} async-done(((bf16[64,64,1024]{2,1,0:T(8,128)(2,1)}), bf16[64,64,1024]{2,1,0:T(8,128)(2,1)}, u32[]{:S(2)}, u32[]{:S(2)}) %all-to-all-start) | async-done | bytes 8388640 | tf_op jit(solution)/shard_map/all_to_all | solution.py:50
  229.8 8.4 %copy.17 = bf16[8,8,64,1024]{3,2,1,0:T(8,128)(2,1)} copy(bf16[8,8,64,1024]{3,2,0,1:T(8,128)(2,1)} %bitcast.5) | data formatting | bytes 16777216 | tf_op jit(solution)/shard_map/all_to_all | solution.py:50
  238.2 7.7 %fusion.4 = bf16[8,256,1024]{2,1,0:T(8,128)(2,1)} fusion(bf16[8,512,1024]{2,1,0:T(8,128)(2,1)} %bitcast.22, s32[8,512]{1,0:T(8,128)S(1)} %eq.34), kind=kOutput, calls=%fused_computation.13 | convolution fusion | flops 2150629376 | bytes 12599296 | tf_op jit(solution)/shard_map/xnt,xni->xti/dot_general | solution.py:19
  245.9 0.0 reduce-scatter.2.cloned.1.call-update
  245.9 3.1 multiply_reduce_fusion.1
  249.0 6.0 %multiply_reduce_fusion = f32[8,8,64]{2,0,1:T(8,128)S(1)} fusion(bf16[8,8,64,1024]{3,2,0,1:T(8,128)(2,1)} %bitcast.5), kind=kLoop, calls=%fused_computation.3 | loop fusion | flops 12578816 | bytes 8404992 | tf_op jit(solution)/shard_map/reduce_sum | solution.py:11
  255.0 0.1 sub.10
  255.1 7.3 %multiply_convert_fusion = bf16[8,512,256]{2,1,0:T(8,128)(2,1)S(1)} fusion(bf16[8,512,1024]{2,1,0:T(8,128)(2,1)} %bitcast.23, bf16[8,256,1024]{2,1,0:T(8,128)(2,1)} %bitcast.25, f32[8,256]{1,0:T(8,128)S(1)} %add.38, f32[8,512]{1,0:T(8,128)S(1)} %sub.10), kind=kOutput, calls=%fused_computation.10 | convolution fusion | flops 2152726528 | bytes 14704640 | tf_op jit(solution)/shard_map/nzy,nvy->nzv/dot_general | solution.py:12
  262.4 2.5 copy.18
  264.9 3.9 %all-to-all-start.1 = ((bf16[8,512,256]{2,0,1:T(8,128)(2,1)}), bf16[8,512,256]{2,0,1:T(8,128)(2,1)S(1)}, u32[]{:S(2)}, u32[]{:S(2)}) async-start(bf16[8,512,256]{2,0,1:T(8,128)(2,1)} %copy.18), calls=%async_computation.1 | async-start | bytes 4194304 | tf_op jit(solution)/shard_map/all_to_all | solution.py:57
  268.8 0.5 convert_reduce_fusion
  269.3 7.7 %psum.7 = f32[2048]{0:T(1024)S(1)} all-reduce(f32[2048]{0:T(1024)S(1)} %bitcast.33), channel_id=1, replica_groups=mesh['grp'=4,'dev'=8] {'grp'}, use_global_device_ids=true, to_apply=%region_7.8 | all-reduce | flops 2048 | bytes 16384 | tf_op jit(solution)/shard_map/psum | solution.py:62
  277.1 40.2 %all-to-all-done.1 = bf16[8,512,256]{2,0,1:T(8,128)(2,1)S(1)} async-done(((bf16[8,512,256]{2,0,1:T(8,128)(2,1)}), bf16[8,512,256]{2,0,1:T(8,128)(2,1)S(1)}, u32[]{:S(2)}, u32[]{:S(2)}) %all-to-all-start.1) | async-done | bytes 2097184 | tf_op jit(solution)/shard_map/all_to_all | solution.py:57
  317.3 0.0 copy-start
  317.3 1.3 copy-done
  318.6 2.1 copy.19
  320.7 9.1 %gather_fusion = bf16[2048,256]{1,0:T(8,128)(2,1)} fusion(bf16[4096,256]{1,0:T(8,128)(2,1)S(1)} %bitcast.20, s32[2048]{0:T(1024)S(1)} %broadcast_clamp_fusion), kind=kCustom, calls=%fused_computation | custom fusion | bytes 2105344 | tf_op jit(solution)/shard_map/gather | solution.py:58
  329.8 0.0 reduce-scatter.2.cloned.1.call-done
  329.8 3.2 add_divide_fusion
  (8 shorter events, 0.1 us)
Async XLA Ops:
  7.2 2.5 copy-start.1
  18.7 22.6 %all-to-all-start.2 = ((s32[8,1,512]{2,1,0:T(1,128)}), s32[8,1,512]{2,1,0:T(1,128)S(1)}, u32[]{:S(2)}, u32[]{:S(2)}) async-start(s32[8,1,512]{2,1,0:T(1,128)} %reshape.73), calls=%async_computation.2 | async-start | bytes 32768 | tf_op jit(solution)/shard_map/all_to_all | solution.py:51
  41.2 188.6 %all-to-all-start = ((bf16[64,64,1024]{2,1,0:T(8,128)(2,1)}), bf16[64,64,1024]{2,1,0:T(8,128)(2,1)}, u32[]{:S(2)}, u32[]{:S(2)}) async-start(bf16[64,64,1024]{2,1,0:T(8,128)(2,1)} %bitcast.21), calls=%async_computation | async-start | bytes 16777216 | tf_op jit(solution)/shard_map/all_to_all | solution.py:50
  47.2 282.5 %reduce-scatter.2.cloned.1.call-start = ((), (), s32[]{:S(2)}) async-start(), calls=%async_computation.4 | async-start | bytes 5242880 | tf_op jit(solution)/shard_map/reduce_scatter | solution.py:59
  264.9 52.4 %all-to-all-start.1 = ((bf16[8,512,256]{2,0,1:T(8,128)(2,1)}), bf16[8,512,256]{2,0,1:T(8,128)(2,1)S(1)}, u32[]{:S(2)}, u32[]{:S(2)}) async-start(bf16[8,512,256]{2,0,1:T(8,128)(2,1)} %copy.18), calls=%async_computation.1 | async-start | bytes 4194304 | tf_op jit(solution)/shard_map/all_to_all | solution.py:57
  317.3 1.3 copy-start
Sparse Core Ops, SparseCore 0:
  246.1 43.6 reduce-scatter.1
where the time goes:
time: 340 us
  waiting for transfers between devices  221 us (65%)
  local copies, waits for them, and re-layouts  48.4 us (14%)
  starting transfers between devices  17.5 us (5%)
  matrix products  17.4 us (5%)
  between operations  14.1 us (4%)
  other arithmetic  13.4 us (4%)
  blocking collectives  7.71 us (2%)
    all_to_all x1, waiting for transfers between devices, shards(): lax.all_to_all(outgoing, 'dev', split_axis=0, concat_axis=1, tiled=True)  181 us
    all_to_all x1, waiting for transfers between devices, shards(): lax.all_to_all(dists, 'dev', split_axis=1, concat_axis=0, tiled=True)  40.2 us
    scatter x1, local copies, waits for them, and re-layouts, shards(): jnp.zeros((nblocks * depth, width), jnp.bfloat16).at[slots].set(points)  15.2 us
    gather x1, local copies, waits for them, and re-layouts, shards(): distances = returned.reshape(nblocks * depth, block_size)[slots]  9.06 us
    all_to_all x1, local copies, waits for them, and re-layouts, shards(): lax.all_to_all(outgoing, 'dev', split_axis=0, concat_axis=1, tiled=True)  8.39 us
    scatter x1, local copies, waits for them, and re-layouts, shards(): targets = jnp.full((nblocks * depth,), -1, jnp.int32).at[slots].set(finals)  8.23 us
    psum x1, blocking collectives, shards(): all_counts = lax.psum(counts, 'grp')  7.71 us
    dot_general x1, matrix products, block_work(): jnp.einsum('xnt,xni->xti', onehot_assign.astype(jnp.bfloat16), received_p...  7.67 us
  transfers between devices with their start and end apart: 4, of which 2 were waited for; matrix products, arithmetic and copies ran while one was open for 14% of the time, Pallas kernels for 0%

commit v1 on v0

--- a/solution.py
+++ b/solution.py
@@ -47,7 +47,12 @@
     outgoing = outgoing.reshape(nblocks, depth, width)
     targets = targets.reshape(nblocks, depth)
     received_points, wanted = (
-        lax.all_to_all(outgoing, "dev", split_axis=0, concat_axis=1, tiled=True),
+        jnp.concatenate(
+            lax.all_to_all(
+                jnp.stack(jnp.split(outgoing, lax.axis_size("dev"), axis=0)), "dev", 0, 0
+            ),
+            axis=1,
+        ),
         lax.all_to_all(targets, "dev", split_axis=0, concat_axis=1, tiled=True),
     )
     centroid_table = centroids.reshape(owned, block_size, width)

time: 340 us -> 354 us (1.041)
  local copies, waits for them, and re-layouts: 48.4 us -> 60.8 us
    all_to_all x1 -> x0, local copies, waits for them, and re-layouts: 8.39 us -> none  [shards(): lax.all_to_all(outgoing, 'dev', split_axis=0, concat_axis=1, tiled=True)]
    reshape x0 -> x1, local copies, waits for them, and re-layouts: none -> 8.39 us  [shards(): jnp.concatenate(lax.all_to_all(jnp.stack(jnp.split(outgoing, lax.axis_siz...]
    unnamed x7 -> x12, local copies, waits for them, and re-layouts: 2.1 us -> 9.56 us
    split x0 -> x1, local copies, waits for them, and re-layouts: none -> 3.89 us  [shards(): jnp.split(outgoing, lax.axis_size('dev'), axis=0)]
  transfers between devices with their start and end apart: 4 -> 4, of which waited for: 2 -> 2; matrix products, arithmetic and copies ran while one was open for 14% -> 17% of each run, Pallas kernels for 0% -> 0%
where the time goes in v1:
time: 354 us; the launch traced here: 353 us
  waiting for transfers between devices  221 us (62%)
  local copies, waits for them, and re-layouts  60.8 us (17%)
  starting transfers between devices  17.5 us (5%)
  matrix products  17.4 us (5%)
  other arithmetic  14.1 us (4%)
  between operations  14.1 us (4%)
  blocking collectives  7.71 us (2%)
    all_to_all x1, waiting for transfers between devices, shards(): lax.all_to_all(jnp.stack(jnp.split(outgoing, lax.axis_size('dev'), axis=0...  181 us
    all_to_all x1, waiting for transfers between devices, shards(): lax.all_to_all(dists, 'dev', split_axis=1, concat_axis=0, tiled=True)  40.2 us
    scatter x1, local copies, waits for them, and re-layouts, shards(): jnp.zeros((nblocks * depth, width), jnp.bfloat16).at[slots].set(points)  15.3 us
    unnamed x12, local copies, waits for them, and re-layouts  9.56 us
    gather x1, local copies, waits for them, and re-layouts, shards(): distances = returned.reshape(nblocks * depth, block_size)[slots]  9.06 us
    reshape x1, local copies, waits for them, and re-layouts, shards(): jnp.concatenate(lax.all_to_all(jnp.stack(jnp.split(outgoing, lax.axis_siz...  8.39 us
    scatter x1, local copies, waits for them, and re-layouts, shards(): targets = jnp.full((nblocks * depth,), -1, jnp.int32).at[slots].set(finals)  8.23 us
    psum x1, blocking collectives, shards(): all_counts = lax.psum(counts, 'grp')  7.71 us
  transfers between devices with their start and end apart: 4, of which 2 were waited for; matrix products, arithmetic and copies ran while one was open for 17% of the time, Pallas kernels for 0%

profile of v1, /device:TPU:0, one launch (start us, length us, event | category | flops | bytes accessed | tf_op | source)
XLA Modules:
  0.0 352.9 jit_solution(4652592949994320993)
XLA Ops:
  7.2 2.4 fusion.7
  9.6 0.7 compare_select_fusion
  10.3 8.2 %scatter_custom_fusion.1 = s32[4096]{0:T(1024)S(1)} fusion(s32[2048]{0:T(1024)S(1)} %bitcast.41, s32[2048]{0:T(1024)} %param.6, s32[]{:T(128)} %constant.8.clone.1), kind=kCustom, calls=%fused_computation.29 | custom fusion | bytes 16896 | tf_op jit(solution)/shard_map/scatter | solution.py:46
  18.6 0.1 all_to_all.30
  18.6 0.7 reshape.94
  19.3 7.3 %all-to-all-start.2 = ((s32[8,1,512]{2,1,0:T(1,128)}), s32[8,1,512]{2,1,0:T(1,128)S(1)}, u32[]{:S(2)}, u32[]{:S(2)}) async-start(s32[8,1,512]{2,1,0:T(1,128)} %reshape.94), calls=%async_computation.2 | async-start | bytes 32768 | tf_op jit(solution)/shard_map/all_to_all | solution.py:56
  26.6 15.3 %scatter_custom_fusion = bf16[4096,1024]{1,0:T(8,128)(2,1)} fusion(s32[2048]{0:T(1024)S(1)} %bitcast.42, bf16[2048,1024]{1,0:T(8,128)(2,1)} %param.4, bf16[]{:T(256)} %constant.12.clone.1), kind=kCustom, calls=%fused_computation.11 | custom fusion | bytes 8389120 | tf_op jit(solution)/shard_map/scatter | solution.py:45
  41.9 3.9 %fusion.11 = (bf16[512,1024]{1,0:T(8,128)(2,1)S(1)}, bf16[512,1024]{1,0:T(8,128)(2,1)S(1)}, bf16[512,1024]{1,0:T(8,128)(2,1)S(1)}, bf16[512,1024]{1,0:T(8,128)(2...) fusion(bf16[4096,1024]{1,0:T(8,128)(2,1)} %scatter_custom_fusion), kind=kLoop, calls=%fused_computation.33 | loop fusion | bytes 16777216 | tf_op jit(solution)/shard_map/split | solution.py:52
  45.8 1.1 constant_dynamic-update-slice_fusion.7
  46.9 1.0 constant_dynamic-update-slice_fusion.6
  48.0 1.0 constant_dynamic-update-slice_fusion.5
  49.0 1.0 constant_dynamic-update-slice_fusion.4
  50.1 1.1 constant_dynamic-update-slice_fusion.3
  51.2 1.0 constant_dynamic-update-slice_fusion.2
  52.2 1.0 constant_dynamic-update-slice_fusion.1
  53.3 1.1 constant_dynamic-update-slice_fusion
  54.3 0.0 all-to-all-done.2
  54.3 6.0 %all-to-all-start = ((bf16[8,8,64,1024]{3,2,1,0:T(8,128)(2,1)}), bf16[8,8,64,1024]{3,2,1,0:T(8,128)(2,1)}, u32[]{:S(2)}, u32[]{:S(2)}) async-start(bf16[8,8,64,1024]{3,2,1,0:T(8,128)(2,1)} %constant_dynamic-update-slice_fusion), calls=%async_computation | async-start | bytes 16777216 | tf_op jit(solution)/shard_map/all_to_all | solution.py:51
  60.3 0.2 reduce-scatter.2.cloned.1.call-start
  60.6 0.5 broadcast.19
  61.1 0.7 reduce.2
  61.8 0.1 reshape.95
  61.9 0.1 eq.34
  61.9 181.0 %all-to-all-done = bf16[8,8,64,1024]{3,2,1,0:T(8,128)(2,1)} async-done(((bf16[8,8,64,1024]{3,2,1,0:T(8,128)(2,1)}), bf16[8,8,64,1024]{3,2,1,0:T(8,128)(2,1)}, u32[]{:S(2)}, u32[]{:S(2)}) %all-to-all-start) | async-done | bytes 8388640 | tf_op jit(solution)/shard_map/all_to_all | solution.py:51
  242.9 8.4 %copy.35 = bf16[8,8,64,1024]{3,2,1,0:T(8,128)(2,1)} copy(bf16[8,8,64,1024]{3,2,0,1:T(8,128)(2,1)} %bitcast.11) | data formatting | bytes 16777216 | tf_op jit(solution)/shard_map/reshape | solution.py:50
  251.3 7.7 %fusion.4 = bf16[8,256,1024]{2,1,0:T(8,128)(2,1)} fusion(bf16[8,512,1024]{2,1,0:T(8,128)(2,1)} %bitcast.27, s32[8,512]{1,0:T(8,128)S(1)} %eq.34), kind=kOutput, calls=%fused_computation.13 | convolution fusion | flops 2150629376 | bytes 12599296 | tf_op jit(solution)/shard_map/xnt,xni->xti/dot_general | solution.py:19
  259.0 0.0 reduce-scatter.2.cloned.1.call-update
  259.0 3.1 multiply_reduce_fusion.1
  262.1 6.0 %multiply_reduce_fusion = f32[8,8,64]{2,0,1:T(8,128)S(1)} fusion(bf16[8,8,64,1024]{3,2,1,0:T(8,128)(2,1)} %all-to-all-done), kind=kLoop, calls=%fused_computation.3 | loop fusion | flops 12578816 | bytes 8404992 | tf_op jit(solution)/shard_map/reduce_sum | solution.py:11
  268.1 0.1 sub.10
  268.2 7.3 %multiply_convert_fusion = bf16[8,512,256]{2,1,0:T(8,128)(2,1)S(1)} fusion(bf16[8,512,1024]{2,1,0:T(8,128)(2,1)} %bitcast.28, bf16[8,256,1024]{2,1,0:T(8,128)(2,1)} %bitcast.30, f32[8,256]{1,0:T(8,128)S(1)} %add.38, f32[8,512]{1,0:T(8,128)S(1)} %sub.10), kind=kOutput, calls=%fused_computation.10 | convolution fusion | flops 2152726528 | bytes 14704640 | tf_op jit(solution)/shard_map/nzy,nvy->nzv/dot_general | solution.py:12
  275.5 2.5 copy.36
  278.0 3.9 %all-to-all-start.1 = ((bf16[8,512,256]{2,0,1:T(8,128)(2,1)}), bf16[8,512,256]{2,0,1:T(8,128)(2,1)S(1)}, u32[]{:S(2)}, u32[]{:S(2)}) async-start(bf16[8,512,256]{2,0,1:T(8,128)(2,1)} %copy.36), calls=%async_computation.1 | async-start | bytes 4194304 | tf_op jit(solution)/shard_map/all_to_all | solution.py:62
  281.9 0.5 convert_reduce_fusion
  282.4 7.7 %psum.7 = f32[2048]{0:T(1024)S(1)} all-reduce(f32[2048]{0:T(1024)S(1)} %bitcast.46), channel_id=1, replica_groups=mesh['grp'=4,'dev'=8] {'grp'}, use_global_device_ids=true, to_apply=%region_7.8 | all-reduce | flops 2048 | bytes 16384 | tf_op jit(solution)/shard_map/psum | solution.py:67
  290.2 40.2 %all-to-all-done.1 = bf16[8,512,256]{2,0,1:T(8,128)(2,1)S(1)} async-done(((bf16[8,512,256]{2,0,1:T(8,128)(2,1)}), bf16[8,512,256]{2,0,1:T(8,128)(2,1)S(1)}, u32[]{:S(2)}, u32[]{:S(2)}) %all-to-all-start.1) | async-done | bytes 2097184 | tf_op jit(solution)/shard_map/all_to_all | solution.py:62
  330.4 0.0 copy-start
  330.4 1.3 copy-done
  331.7 2.1 copy.37
  333.8 9.1 %gather_fusion = bf16[2048,256]{1,0:T(8,128)(2,1)} fusion(bf16[4096,256]{1,0:T(8,128)(2,1)S(1)} %bitcast.26, s32[2048]{0:T(1024)S(1)} %broadcast_clamp_fusion), kind=kCustom, calls=%fused_computation | custom fusion | bytes 2105344 | tf_op jit(solution)/shard_map/gather | solution.py:63
  342.9 0.0 reduce-scatter.2.cloned.1.call-done
  342.9 3.2 add_divide_fusion
  (7 shorter events, 0.0 us)
Async XLA Ops:
  19.3 35.0 %all-to-all-start.2 = ((s32[8,1,512]{2,1,0:T(1,128)}), s32[8,1,512]{2,1,0:T(1,128)S(1)}, u32[]{:S(2)}, u32[]{:S(2)}) async-start(s32[8,1,512]{2,1,0:T(1,128)} %reshape.94), calls=%async_computation.2 | async-start | bytes 32768 | tf_op jit(solution)/shard_map/all_to_all | solution.py:56
  54.3 188.6 %all-to-all-start = ((bf16[8,8,64,1024]{3,2,1,0:T(8,128)(2,1)}), bf16[8,8,64,1024]{3,2,1,0:T(8,128)(2,1)}, u32[]{:S(2)}, u32[]{:S(2)}) async-start(bf16[8,8,64,1024]{3,2,1,0:T(8,128)(2,1)} %constant_dynamic-update-slice_fusion), calls=%async_computation | async-start | bytes 16777216 | tf_op jit(solution)/shard_map/all_to_all | solution.py:51
  60.3 282.5 %reduce-scatter.2.cloned.1.call-start = ((), (), s32[]{:S(2)}) async-start(), calls=%async_computation.4 | async-start | bytes 5242880 | tf_op jit(solution)/shard_map/reduce_scatter | solution.py:64
  278.0 52.4 %all-to-all-start.1 = ((bf16[8,512,256]{2,0,1:T(8,128)(2,1)}), bf16[8,512,256]{2,0,1:T(8,128)(2,1)S(1)}, u32[]{:S(2)}, u32[]{:S(2)}) async-start(bf16[8,512,256]{2,0,1:T(8,128)(2,1)} %copy.36), calls=%async_computation.1 | async-start | bytes 4194304 | tf_op jit(solution)/shard_map/all_to_all | solution.py:62
  330.4 1.3 copy-start
Sparse Core Ops, SparseCore 0:
  259.1 43.7 reduce-scatter.1
